TPU v7x, 32 devices: a whole 2x2x4 slice. The times are simulated.
32 devices in a mesh: row: 8 (over z, y), col: 4 (over x, core).
Axes of the slice: x: 2, y: 2, z: 4, core: 2. Of those that a mesh axis runs over, the one named last changes fastest.
Arguments:
- matrix: float32 [4096, 4096], P('row', 'col'), may hold values from -0.92 to 1.92, as said below
Outputs:
- inverse: float32 [4096, 4096], P('row', 'col')
- residual_norms: float32 [4], replicated
Inputs may be any that keep to these rules, and one draw needn't show every extreme that they name: matrix is exactly symmetric and positive definite; all its eigenvalues lie between 0.08 and 1.92.
All inputs are finite; a program needn't handle non-finite values.
Results may differ from a plain program's by a relative error of at most 0.0017.
The roundings to bfloat16 on the way count: a program that leaves them out, or rounds other values in their place, can miss the bound.
Values may be sent and summed in bfloat16 or wider, within the bound.
A program may use at most 64 MiB of HBM per device.

v0:
```python
import jax
import jax.numpy as jnp
from jax import lax
from jax.sharding import PartitionSpec as P

N = 4096
ITERS = 4


def shards(matrix):
    row_count, col_count = matrix.shape
    row_index = lax.axis_index("row")
    col_index = lax.axis_index("col")
    sq_total = lax.psum(jnp.sum(matrix * matrix), ("row", "col"))
    start_scale = jnp.sqrt(jnp.float32(N)) / jnp.sqrt(sq_total)
    global_rows = row_index * row_count + lax.broadcasted_iota(jnp.int32, (row_count, col_count), 0)
    global_cols = col_index * col_count + lax.broadcasted_iota(jnp.int32, (row_count, col_count), 1)
    eye_block = (global_rows == global_cols).astype(jnp.float32)
    mat_low = matrix.astype(jnp.bfloat16)
    panel_rows = lax.all_gather(mat_low, "col", axis=1, tiled=True)
    current = start_scale * eye_block
    partial_list = []
    for iteration in range(ITERS):
        cur_low = current.astype(jnp.bfloat16)
        product = jnp.dot(
            panel_rows,
            lax.all_gather(cur_low, "row", axis=0, tiled=True),
            preferred_element_type=jnp.float32,
        )
        residual = eye_block - product
        local_sum = jnp.sum(residual * residual)
        partial_list.append(local_sum)
        shift_low = (eye_block + residual).astype(jnp.bfloat16)
        iterate_rows = lax.all_gather(cur_low, "col", axis=1, tiled=True)
        current = jnp.dot(
            iterate_rows,
            lax.all_gather(shift_low, "row", axis=0, tiled=True),
            preferred_element_type=jnp.float32,
        )
    summed = lax.psum(jnp.stack(partial_list), ("row", "col"))
    residual_norms = jnp.sqrt(summed / N)
    return (current, residual_norms)


def solution(mesh):
    in_specs = (P("row", "col"),)
    out_specs = (P("row", "col"), P())
    return jax.shard_map(shards, mesh=mesh, in_specs=in_specs, out_specs=out_specs, check_vma=False)
```

profile of v0, /device:TPU:0, one launch (start us, length us, event | category | flops | bytes accessed | tf_op | source)
XLA Modules:
  0.0 1244.2 jit_solution(14768718448786911574)
XLA Ops:
  7.2 0.0 all-gather.18.cloned.1.call-start
  7.2 4.3 fusion.5
  11.5 0.0 all-gather.18.cloned.1.call-update
  11.5 0.0 all-gather.16.cloned.1.call-start
  11.6 42.5 %psum.14 = f32[]{:T(128)} all-reduce(f32[]{:T(128)} %get-tuple-element.8), channel_id=1, replica_groups=mesh['row'=8,'col'=4] {'row','col'}, use_global_device_ids=true, to_apply=%region_1.0 | all-reduce | flops 1 | bytes 8 | tf_op jit(solution)/shard_map/psum | solution.py:14
  54.8 1.2 fusion
  56.0 0.0 all-gather.16.cloned.1.call-update
  56.1 0.0 all-gather.14.cloned.1.call-start
  56.1 0.7 all-gather.14.cloned.1.call-update
  56.8 0.0 all-gather.20.cloned.1.call-start
  56.9 0.0 all-gather.18.cloned.1.call-done
  56.9 124.6 %all-gather.16.cloned.1.call-done = bf16[4096,1024]{0,1:T(8,128)(2,1)} async-done(((bf16[512,1024]{0,1:T(8,128)(2,1)}), bf16[4096,1024]{0,1:T(8,128)(2,1)}) %all-gather.16.cloned.1.call-update) | async-done | bytes 8388624 | tf_op jit(solution)/shard_map/all_gather | solution.py:27
  181.5 10.1 fusion.1
  191.6 0.0 all-gather.20.cloned.1.call-update
  191.6 0.0 all-gather.24.cloned.1.call-start
  191.7 24.1 %all-gather.14.cloned.1.call-done = bf16[512,4096]{0,1:T(8,128)(2,1)} async-done(((bf16[512,1024]{0,1:T(8,128)(2,1)}), bf16[512,4096]{0,1:T(8,128)(2,1)}) %all-gather.14.cloned.1.call-update) | async-done | bytes 4194320 | tf_op jit(solution)/shard_map/all_gather | solution.py:34
  215.7 127.4 %all-gather.20.cloned.1.call-done = bf16[4096,1024]{0,1:T(8,128)(2,1)} async-done(((bf16[512,1024]{0,1:T(8,128)(2,1)}), bf16[4096,1024]{0,1:T(8,128)(2,1)}) %all-gather.20.cloned.1.call-update) | async-done | bytes 8388624 | tf_op jit(solution)/shard_map/all_gather | solution.py:37
  343.2 10.2 convolution_convert_fusion.2
  353.4 0.0 all-gather.24.cloned.1.call-update
  353.4 0.0 all-gather.22.cloned.1.call-start
  353.4 0.5 all-gather.22.cloned.1.call-update
  354.0 0.5 all-gather.26.cloned.1.call-start
  354.5 121.7 %all-gather.24.cloned.1.call-done = bf16[4096,1024]{1,0:T(8,128)(2,1)} async-done(((bf16[512,1024]{1,0:T(8,128)(2,1)}), bf16[4096,1024]{1,0:T(8,128)(2,1)}) %all-gather.24.cloned.1.call-update) | async-done | bytes 8388624 | tf_op jit(solution)/shard_map/all_gather | solution.py:27
  476.2 10.9 fusion.2
  487.1 0.0 all-gather.26.cloned.1.call-update
  487.1 0.0 all-gather.30.cloned.1.call-start
  487.1 23.1 %all-gather.22.cloned.1.call-done = bf16[512,4096]{1,0:T(8,128)(2,1)} async-done(((bf16[512,1024]{1,0:T(8,128)(2,1)}), bf16[512,4096]{1,0:T(8,128)(2,1)}) %all-gather.22.cloned.1.call-update) | async-done | bytes 4194320 | tf_op jit(solution)/shard_map/all_gather | solution.py:34
  510.3 127.0 %all-gather.26.cloned.1.call-done = bf16[4096,1024]{0,1:T(8,128)(2,1)} async-done(((bf16[512,1024]{0,1:T(8,128)(2,1)}), bf16[4096,1024]{0,1:T(8,128)(2,1)}) %all-gather.26.cloned.1.call-update) | async-done | bytes 8388624 | tf_op jit(solution)/shard_map/all_gather | solution.py:37
  637.3 10.2 convolution_convert_fusion.1
  647.5 0.0 all-gather.28.cloned.1.call-start
  647.5 0.7 all-gather.28.cloned.1.call-update
  648.2 0.2 all-gather.32.cloned.1.call-start
  648.4 121.9 %all-gather.30.cloned.1.call-done = bf16[4096,1024]{1,0:T(8,128)(2,1)} async-done(((bf16[512,1024]{1,0:T(8,128)(2,1)}), bf16[4096,1024]{1,0:T(8,128)(2,1)}) %all-gather.30.cloned.1.call-update) | async-done | bytes 8388624 | tf_op jit(solution)/shard_map/all_gather | solution.py:27
  770.3 10.9 fusion.3
  781.2 0.0 all-gather.36.cloned.1.call-start
  781.2 23.3 %all-gather.28.cloned.1.call-done = bf16[512,4096]{1,0:T(8,128)(2,1)} async-done(((bf16[512,1024]{1,0:T(8,128)(2,1)}), bf16[512,4096]{1,0:T(8,128)(2,1)}) %all-gather.28.cloned.1.call-update) | async-done | bytes 4194320 | tf_op jit(solution)/shard_map/all_gather | solution.py:34
  804.5 126.9 %all-gather.32.cloned.1.call-done = bf16[4096,1024]{0,1:T(8,128)(2,1)} async-done(((bf16[512,1024]{0,1:T(8,128)(2,1)}), bf16[4096,1024]{0,1:T(8,128)(2,1)}) %all-gather.32.cloned.1.call-update) | async-done | bytes 8388624 | tf_op jit(solution)/shard_map/all_gather | solution.py:37
  931.4 10.2 convolution_convert_fusion
  941.6 0.0 all-gather.34.cloned.1.call-start
  941.6 0.5 all-gather.34.cloned.1.call-update
  942.2 0.3 all-gather.38.cloned.1.call-start
  942.4 122.0 %all-gather.36.cloned.1.call-done = bf16[4096,1024]{1,0:T(8,128)(2,1)} async-done(((bf16[512,1024]{1,0:T(8,128)(2,1)}), bf16[4096,1024]{1,0:T(8,128)(2,1)}) %all-gather.36.cloned.1.call-update) | async-done | bytes 8388624 | tf_op jit(solution)/shard_map/all_gather | solution.py:27
  1064.4 12.9 %multiply_reduce_fusion.3 = (f32[]{:T(128)}, f32[]{:T(128)}, f32[]{:T(128)}, f32[]{:T(128)}, bf16[512,1024]{0,1:T(8,128)(2,1)}) fusion(f32[1024,512]{1,0:T(8,128)S(1)} %get-tuple-element.10, s32[512]{0:T(512)S(1)} %iota_add_fusion.1, s32[1024]{0:T(1024)S(1)} %iota_add_fusion, f32[1024,512]{1,0:T(8,128)} %get-tuple-element.12, ...), kind=kOutput, calls=%fused_computation.17 | convolution fusion | flops 4303355904 | bytes 19929104 | tf_op jit(solution)/shard_map/dot_general | solution.py:25
  1077.4 2.6 pad_maximum_fusion
  1079.9 39.1 %psum.15 = f32[4]{0:T(128)S(1)} all-reduce(f32[4]{0:T(128)S(1)} %pad_maximum_fusion), channel_id=1, replica_groups=mesh['row'=8,'col'=4] {'row','col'}, use_global_device_ids=true, to_apply=%region_6.0 | all-reduce | flops 4 | bytes 32 | tf_op jit(solution)/shard_map/psum | solution.py:40
  1119.1 0.5 multiply_sqrt_fusion
  1119.6 107.3 %all-gather.38.cloned.1.call-done = bf16[4096,1024]{0,1:T(8,128)(2,1)} async-done(((bf16[512,1024]{0,1:T(8,128)(2,1)}), bf16[4096,1024]{0,1:T(8,128)(2,1)}) %all-gather.38.cloned.1.call-update) | async-done | bytes 8388624 | tf_op jit(solution)/shard_map/all_gather | solution.py:37
  1226.9 10.5 fusion.6
  (7 shorter events, 0.1 us)
Async XLA Ops:
  7.2 49.7 %all-gather.18.cloned.1.call-start = ((), (), s32[]{:S(2)}) async-start(), calls=%async_computation.2 | async-start | bytes 5242880 | tf_op jit(solution)/shard_map/all_gather | solution.py:20
  11.5 170.0 %all-gather.16.cloned.1.call-start = ((), (), s32[]{:S(2)}) async-start(), calls=%async_computation.1 | async-start | bytes 9437184 | tf_op jit(solution)/shard_map/all_gather | solution.py:27
  56.1 159.7 %all-gather.14.cloned.1.call-start = ((), (), s32[]{:S(2)}) async-start(), calls=%async_computation | async-start | bytes 5242880 | tf_op jit(solution)/shard_map/all_gather | solution.py:34
  56.8 286.4 %all-gather.20.cloned.1.call-start = ((), (), s32[]{:S(2)}) async-start(), calls=%async_computation.3 | async-start | bytes 9437184 | tf_op jit(solution)/shard_map/all_gather | solution.py:37
  191.6 284.6 %all-gather.24.cloned.1.call-start = ((), (), s32[]{:S(2)}) async-start(), calls=%async_computation.5 | async-start | bytes 9437184 | tf_op jit(solution)/shard_map/all_gather | solution.py:27
  353.4 156.9 %all-gather.22.cloned.1.call-start = ((), (), s32[]{:S(2)}) async-start(), calls=%async_computation.4 | async-start | bytes 5242880 | tf_op jit(solution)/shard_map/all_gather | solution.py:34
  354.0 283.3 %all-gather.26.cloned.1.call-start = ((), (), s32[]{:S(2)}) async-start(), calls=%async_computation.6 | async-start | bytes 9437184 | tf_op jit(solution)/shard_map/all_gather | solution.py:37
  487.1 283.2 %all-gather.30.cloned.1.call-start = ((), (), s32[]{:S(2)}) async-start(), calls=%async_computation.8 | async-start | bytes 9437184 | tf_op jit(solution)/shard_map/all_gather | solution.py:27
  647.5 157.0 %all-gather.28.cloned.1.call-start = ((), (), s32[]{:S(2)}) async-start(), calls=%async_computation.7 | async-start | bytes 5242880 | tf_op jit(solution)/shard_map/all_gather | solution.py:34
  648.2 283.2 %all-gather.32.cloned.1.call-start = ((), (), s32[]{:S(2)}) async-start(), calls=%async_computation.9 | async-start | bytes 9437184 | tf_op jit(solution)/shard_map/all_gather | solution.py:37
  781.2 283.2 %all-gather.36.cloned.1.call-start = ((), (), s32[]{:S(2)}) async-start(), calls=%async_computation.11 | async-start | bytes 9437184 | tf_op jit(solution)/shard_map/all_gather | solution.py:27
  941.6 178.0 %all-gather.34.cloned.1.call-start = ((), (), s32[]{:S(2)}) async-start(), calls=%async_computation.10 | async-start | bytes 5242880 | tf_op jit(solution)/shard_map/all_gather | solution.py:34
  942.2 284.7 %all-gather.38.cloned.1.call-start = ((), (), s32[]{:S(2)}) async-start(), calls=%async_computation.12 | async-start | bytes 9437184 | tf_op jit(solution)/shard_map/all_gather | solution.py:37
Sparse Core Ops, SparseCore 0:
  11.6 37.4 all-gather.17
  56.2 125.2 all-gather.15
  183.1 32.6 all-gather.13
  218.2 124.9 all-gather.19
  353.5 122.6 all-gather.23
  477.6 32.6 all-gather.21
  512.3 124.9 all-gather.25
  647.6 122.6 all-gather.29
  771.9 32.6 all-gather.27
  806.4 124.9 all-gather.31
  941.7 122.6 all-gather.35
  1065.8 33.3 all-gather.33
  1101.2 125.6 all-gather.37
where the time goes:
time: 1250 us; the launch traced here: 1240 us
  waiting for transfers between devices  1050 us (84%)
  matrix products  85.8 us (7%)
  blocking collectives  81.7 us (7%)
  between operations  14.9 us (1%)
    all_gather x4, waiting for transfers between devices, shards(): lax.all_gather(cur_low, 'row', axis=0, tiled=True)  490 us
    all_gather x4, waiting for transfers between devices, shards(): lax.all_gather(shift_low, 'row', axis=0, tiled=True)  489 us
    all_gather x4, waiting for transfers between devices, shards(): iterate_rows = lax.all_gather(cur_low, 'col', axis=1, tiled=True)  70.5 us
    dot_general x4, matrix products, shards(): jnp.dot(panel_rows, lax.all_gather(cur_low, 'row', axis=0, tiled=True), p...  44.8 us
    psum x1, blocking collectives, shards(): sq_total = lax.psum(jnp.sum(matrix * matrix), ('row', 'col'))  42.5 us
    dot_general x4, matrix products, shards(): jnp.dot(iterate_rows, lax.all_gather(shift_low, 'row', axis=0, tiled=True...  41 us
    psum x1, blocking collectives, shards(): summed = lax.psum(jnp.stack(partial_list), ('row', 'col'))  39.1 us
  transfers between devices with their start and end apart: 13, of which 11 were waited for; matrix products, arithmetic and copies ran while one was open for 4% of the time, Pallas kernels for 0%

commit v1 on v0

--- a/solution.py
+++ b/solution.py
@@ -34,7 +34,9 @@
         iterate_rows = lax.all_gather(cur_low, "col", axis=1, tiled=True)
         current = jnp.dot(
             iterate_rows,
-            lax.all_gather(shift_low, "row", axis=0, tiled=True),
+            jnp.concatenate(
+                lax.all_to_all(jnp.stack([shift_low] * lax.axis_size("row")), "row", 0, 0), axis=0
+            ),
             preferred_element_type=jnp.float32,
         )
     summed = lax.psum(jnp.stack(partial_list), ("row", "col"))

time: 1250 us -> 1440 us (1.15)
  blocking collectives: 81.7 us -> 242 us
  starting transfers between devices: 1.37 us -> 21.2 us
  local copies, waits for them, and re-layouts: 0 us -> 19.4 us
    all_gather x4 -> x0, waiting for transfers between devices: 489 us -> none  [shards(): lax.all_gather(shift_low, 'row', axis=0, tiled=True)]
    all_to_all x0 -> x4, waiting for transfers between devices: none -> 434 us  [shards(): lax.all_to_all(jnp.stack([shift_low] * lax.axis_size('row')), 'row', 0, 0)]
    psum x1, blocking collectives: 39.1 us -> 199 us  [shards(): summed = lax.psum(jnp.stack(partial_list), ('row', 'col'))]
    all_gather x4, waiting for transfers between devices: 70.5 us -> 111 us  [shards(): iterate_rows = lax.all_gather(cur_low, 'col', axis=1, tiled=True)]
    all_to_all x0 -> x4, starting transfers between devices: none -> 19.8 us  [shards(): lax.all_to_all(jnp.stack([shift_low] * lax.axis_size('row')), 'row', 0, 0)]
    another operation x0 -> x4, local copies, waits for them, and re-layouts: none -> 17.3 us  [shards(): jnp.stack([shift_low] * lax.axis_size('row'))]
  transfers between devices with their start and end apart: 13 -> 13, of which waited for: 11 -> 10; matrix products, arithmetic and copies ran while one was open for 4% -> 0% of each run, Pallas kernels for 0% -> 0%
where the time goes in v1:
time: 1440 us; the launch traced here: 1430 us
  waiting for transfers between devices  1040 us (72%)
  blocking collectives  242 us (17%)
  matrix products  84.9 us (6%)
  starting transfers between devices  21.2 us (1%)
  local copies, waits for them, and re-layouts  19.4 us (1%)
  between operations  14.9 us (1%)
    all_gather x4, waiting for transfers between devices, shards(): lax.all_gather(cur_low, 'row', axis=0, tiled=True)  496 us
    all_to_all x4, waiting for transfers between devices, shards(): lax.all_to_all(jnp.stack([shift_low] * lax.axis_size('row')), 'row', 0, 0)  434 us
    psum x1, blocking collectives, shards(): summed = lax.psum(jnp.stack(partial_list), ('row', 'col'))  199 us
    all_gather x4, waiting for transfers between devices, shards(): iterate_rows = lax.all_gather(cur_low, 'col', axis=1, tiled=True)  111 us
    dot_general x4, matrix products, shards(): jnp.dot(panel_rows, lax.all_gather(cur_low, 'row', axis=0, tiled=True), p...  43.9 us
    psum x1, blocking collectives, shards(): sq_total = lax.psum(jnp.sum(matrix * matrix), ('row', 'col'))  42.5 us
    dot_general x4, matrix products, shards(): jnp.dot(iterate_rows, jnp.concatenate(lax.all_to_all(jnp.stack([shift_low...  41 us
  transfers between devices with their start and end apart: 13, of which 10 were waited for; matrix products, arithmetic and copies ran while one was open for 0% of the time, Pallas kernels for 0%

profile of v1, /device:TPU:0, one launch (start us, length us, event | category | flops | bytes accessed | tf_op | source)
XLA Modules:
  0.0 1434.6 jit_solution(6027263705423390062)
XLA Ops:
  7.2 4.3 fusion.5
  11.5 0.0 all-gather.12.cloned.1.call-start
  11.6 42.5 %psum.14 = f32[]{:T(128)} all-reduce(f32[]{:T(128)} %get-tuple-element.8), channel_id=1, replica_groups=mesh['row'=8,'col'=4] {'row','col'}, use_global_device_ids=true, to_apply=%region_1.0 | all-reduce | flops 1 | bytes 8 | tf_op jit(solution)/shard_map/psum | solution.py:14
  54.8 1.3 fusion
  56.2 125.4 %all-gather.12.cloned.1.call-done = bf16[4096,1024]{0,1:T(8,128)(2,1)} async-done(((bf16[512,1024]{0,1:T(8,128)(2,1)}), bf16[4096,1024]{0,1:T(8,128)(2,1)}) %all-gather.12.cloned.1.call-update) | async-done | bytes 8388624 | tf_op jit(solution)/shard_map/all_gather | solution.py:27
  181.5 10.4 fusion.1
  191.9 0.5 copy.3
  192.5 4.3 stack.18
  196.8 5.0 all-to-all-start
  201.8 0.0 all-gather.10.cloned.1.call-start
  201.8 0.7 all-gather.10.cloned.1.call-update
  202.5 0.3 all-gather.18.cloned.1.call-start
  202.8 37.1 %all-gather.10.cloned.1.call-done = bf16[512,4096]{0,1:T(8,128)(2,1)} async-done(((bf16[512,1024]{0,1:T(8,128)(2,1)}), bf16[512,4096]{0,1:T(8,128)(2,1)}) %all-gather.10.cloned.1.call-update) | async-done | bytes 4194320 | tf_op jit(solution)/shard_map/all_gather | solution.py:34
  239.9 144.4 %all-to-all-done = bf16[8,512,1024]{2,1,0:T(8,128)(2,1)} async-done(((bf16[8,512,1024]{2,1,0:T(8,128)(2,1)}), bf16[8,512,1024]{2,1,0:T(8,128)(2,1)}, u32[]{:S(2)}, u32[]{:S(2)}) %all-to-all-start) | async-done | bytes 8388640 | tf_op jit(solution)/shard_map/all_to_all | solution.py:38
  384.3 10.1 convolution_convert_fusion.2
  394.5 123.7 %all-gather.18.cloned.1.call-done = bf16[4096,1024]{1,0:T(8,128)(2,1)} async-done(((bf16[512,1024]{1,0:T(8,128)(2,1)}), bf16[4096,1024]{1,0:T(8,128)(2,1)}) %all-gather.18.cloned.1.call-update) | async-done | bytes 8388624 | tf_op jit(solution)/shard_map/all_gather | solution.py:27
  518.2 10.6 fusion.2
  528.8 0.5 copy.4
  529.4 4.3 stack.19
  533.7 5.0 all-to-all-start.1
  538.6 0.0 all-gather.16.cloned.1.call-start
  538.7 0.5 all-gather.16.cloned.1.call-update
  539.2 0.6 all-gather.22.cloned.1.call-start
  539.8 36.7 %all-gather.16.cloned.1.call-done = bf16[512,4096]{1,0:T(8,128)(2,1)} async-done(((bf16[512,1024]{1,0:T(8,128)(2,1)}), bf16[512,4096]{1,0:T(8,128)(2,1)}) %all-gather.16.cloned.1.call-update) | async-done | bytes 4194320 | tf_op jit(solution)/shard_map/all_gather | solution.py:34
  576.5 144.8 %all-to-all-done.1 = bf16[8,512,1024]{2,1,0:T(8,128)(2,1)} async-done(((bf16[8,512,1024]{2,1,0:T(8,128)(2,1)}), bf16[8,512,1024]{2,1,0:T(8,128)(2,1)}, u32[]{:S(2)}, u32[]{:S(2)}) %all-to-all-start.1) | async-done | bytes 8388640 | tf_op jit(solution)/shard_map/all_to_all | solution.py:38
  721.3 10.2 convolution_convert_fusion.1
  731.5 123.6 %all-gather.22.cloned.1.call-done = bf16[4096,1024]{1,0:T(8,128)(2,1)} async-done(((bf16[512,1024]{1,0:T(8,128)(2,1)}), bf16[4096,1024]{1,0:T(8,128)(2,1)}) %all-gather.22.cloned.1.call-update) | async-done | bytes 8388624 | tf_op jit(solution)/shard_map/all_gather | solution.py:27
  855.1 10.5 fusion.3
  865.7 0.5 copy.5
  866.2 4.3 stack.20
  870.5 5.0 all-to-all-start.2
  875.5 0.0 all-gather.20.cloned.1.call-start
  875.5 0.7 all-gather.20.cloned.1.call-update
  876.2 0.2 all-gather.26.cloned.1.call-start
  876.4 37.2 %all-gather.20.cloned.1.call-done = bf16[512,4096]{1,0:T(8,128)(2,1)} async-done(((bf16[512,1024]{1,0:T(8,128)(2,1)}), bf16[512,4096]{1,0:T(8,128)(2,1)}) %all-gather.20.cloned.1.call-update) | async-done | bytes 4194320 | tf_op jit(solution)/shard_map/all_gather | solution.py:34
  913.6 144.5 %all-to-all-done.2 = bf16[8,512,1024]{2,1,0:T(8,128)(2,1)} async-done(((bf16[8,512,1024]{2,1,0:T(8,128)(2,1)}), bf16[8,512,1024]{2,1,0:T(8,128)(2,1)}, u32[]{:S(2)}, u32[]{:S(2)}) %all-to-all-start.2) | async-done | bytes 8388640 | tf_op jit(solution)/shard_map/all_to_all | solution.py:38
  1058.1 10.2 convolution_convert_fusion
  1068.3 123.6 %all-gather.26.cloned.1.call-done = bf16[4096,1024]{1,0:T(8,128)(2,1)} async-done(((bf16[512,1024]{1,0:T(8,128)(2,1)}), bf16[4096,1024]{1,0:T(8,128)(2,1)}) %all-gather.26.cloned.1.call-update) | async-done | bytes 8388624 | tf_op jit(solution)/shard_map/all_gather | solution.py:27
  1191.9 12.4 multiply_reduce_fusion.3
  1204.3 0.5 copy.6
  1204.8 4.3 stack.21
  1209.2 5.0 all-to-all-start.3
  1214.1 0.0 all-gather.24.cloned.1.call-start
  1214.2 0.7 all-gather.24.cloned.1.call-update
  1214.8 2.5 pad_maximum_fusion
  1217.4 199.5 %psum.15 = f32[4]{0:T(128)S(1)} all-reduce(f32[4]{0:T(128)S(1)} %pad_maximum_fusion), channel_id=1, replica_groups=mesh['row'=8,'col'=4] {'row','col'}, use_global_device_ids=true, to_apply=%region_6.0 | all-reduce | flops 4 | bytes 32 | tf_op jit(solution)/shard_map/psum | solution.py:42
  1416.9 0.5 multiply_sqrt_fusion
  1417.4 10.5 fusion.6
  (11 shorter events, 0.2 us)
Async XLA Ops:
  7.2 49.0 %all-gather.14.cloned.1.call-start = ((), (), s32[]{:S(2)}) async-start(), calls=%async_computation.6 | async-start | bytes 5242880 | tf_op jit(solution)/shard_map/all_gather | solution.py:20
  11.5 170.0 %all-gather.12.cloned.1.call-start = ((), (), s32[]{:S(2)}) async-start(), calls=%async_computation.5 | async-start | bytes 9437184 | tf_op jit(solution)/shard_map/all_gather | solution.py:27
  196.8 187.5 %all-to-all-start = ((bf16[8,512,1024]{2,1,0:T(8,128)(2,1)}), bf16[8,512,1024]{2,1,0:T(8,128)(2,1)}, u32[]{:S(2)}, u32[]{:S(2)}) async-start(bf16[8,512,1024]{2,1,0:T(8,128)(2,1)} %stack.18), calls=%async_computation | async-start | bytes 16777216 | tf_op jit(solution)/shard_map/all_to_all | solution.py:38
  201.8 38.2 %all-gather.10.cloned.1.call-start = ((), (), s32[]{:S(2)}) async-start(), calls=%async_computation.4 | async-start | bytes 5242880 | tf_op jit(solution)/shard_map/all_gather | solution.py:34
  202.5 315.7 %all-gather.18.cloned.1.call-start = ((), (), s32[]{:S(2)}) async-start(), calls=%async_computation.8 | async-start | bytes 9437184 | tf_op jit(solution)/shard_map/all_gather | solution.py:27
  533.7 187.6 %all-to-all-start.1 = ((bf16[8,512,1024]{2,1,0:T(8,128)(2,1)}), bf16[8,512,1024]{2,1,0:T(8,128)(2,1)}, u32[]{:S(2)}, u32[]{:S(2)}) async-start(bf16[8,512,1024]{2,1,0:T(8,128)(2,1)} %stack.19), calls=%async_computation.1 | async-start | bytes 16777216 | tf_op jit(solution)/shard_map/all_to_all | solution.py:38
  538.6 37.8 %all-gather.16.cloned.1.call-start = ((), (), s32[]{:S(2)}) async-start(), calls=%async_computation.7 | async-start | bytes 5242880 | tf_op jit(solution)/shard_map/all_gather | solution.py:34
  539.2 315.9 %all-gather.22.cloned.1.call-start = ((), (), s32[]{:S(2)}) async-start(), calls=%async_computation.10 | async-start | bytes 9437184 | tf_op jit(solution)/shard_map/all_gather | solution.py:27
  870.5 187.6 %all-to-all-start.2 = ((bf16[8,512,1024]{2,1,0:T(8,128)(2,1)}), bf16[8,512,1024]{2,1,0:T(8,128)(2,1)}, u32[]{:S(2)}, u32[]{:S(2)}) async-start(bf16[8,512,1024]{2,1,0:T(8,128)(2,1)} %stack.20), calls=%async_computation.2 | async-start | bytes 16777216 | tf_op jit(solution)/shard_map/all_to_all | solution.py:38
  875.5 38.1 %all-gather.20.cloned.1.call-start = ((), (), s32[]{:S(2)}) async-start(), calls=%async_computation.9 | async-start | bytes 5242880 | tf_op jit(solution)/shard_map/all_gather | solution.py:34
  876.2 315.7 %all-gather.26.cloned.1.call-start = ((), (), s32[]{:S(2)}) async-start(), calls=%async_computation.12 | async-start | bytes 9437184 | tf_op jit(solution)/shard_map/all_gather | solution.py:27
  1209.2 208.3 %all-to-all-start.3 = ((bf16[8,512,1024]{2,1,0:T(8,128)(2,1)}), bf16[8,512,1024]{2,1,0:T(8,128)(2,1)}, u32[]{:S(2)}, u32[]{:S(2)}) async-start(bf16[8,512,1024]{2,1,0:T(8,128)(2,1)} %stack.21), calls=%async_computation.3 | async-start | bytes 16777216 | tf_op jit(solution)/shard_map/all_to_all | solution.py:38
  1214.1 203.3 %all-gather.24.cloned.1.call-start = ((), (), s32[]{:S(2)}) async-start(), calls=%async_computation.11 | async-start | bytes 5242880 | tf_op jit(solution)/shard_map/all_gather | solution.py:34
Sparse Core Ops, SparseCore 0:
  11.6 37.4 all-gather.13
  56.2 125.2 all-gather.11
  204.1 35.7 all-gather.9
  394.6 123.5 all-gather.17
  540.7 35.7 all-gather.15
  731.6 123.4 all-gather.21
  877.8 35.7 all-gather.19
  1068.4 123.4 all-gather.25
  1216.5 35.7 all-gather.23
